TPU v7x, 32 devices: a whole 2x2x4 slice. The times are simulated.
32 devices in a mesh: dp: 8 (over z, y), mp: 4 (over x, core).
Axes of the slice: x: 2, y: 2, z: 4, core: 2. Of those that a mesh axis runs over, the one named last changes fastest.
Arguments:
- queries: bfloat16 [4096, 4096], P('dp', 'mp'), may hold values from -6 to 6
- passages: bfloat16 [4096, 4096], P('dp', 'mp'), may hold values from -6 to 6
- labels: int32 [4096], P('dp'), may hold values from 0 to 4095
- projection: bfloat16 [4096, 128], P('mp'), may hold values from -0.09375 to 0.09375
Outputs:
- loss: float32 [4096], P('dp')
- query_embed: bfloat16 [4096, 128], P('dp')
All inputs are finite; a program needn't handle non-finite values.
Results may differ from a plain program's by a relative error of at most 0.0039.
Values may be sent and summed in bfloat16 or wider, within the bound.
No kernel may reach another device: no remote copies, remote signals or barrier semaphores. Data moves between devices by JAX's collectives and lax.ppermute only.
A program may use at most 64 MiB of HBM per device.

v0:
```python
import jax
import jax.numpy as jnp
from jax import lax
from jax.sharding import PartitionSpec as P


def merged(part, axis, combine):
    gathered = jax.tree.map(lambda a: lax.all_gather(a, axis), part)

    def take(source):
        return jax.tree.map(lambda a: lax.dynamic_index_in_dim(a, source, 0, False), gathered)

    return lax.fori_loop(
        1, lax.axis_size(axis), lambda source, state: combine(state, take(source)), take(0)
    )


def combine_stats(first, second):
    top = jnp.maximum(first[0], second[0])
    total = first[1] * jnp.exp(first[0] - top) + second[1] * jnp.exp(second[0] - top)
    return (top, total, first[2] + second[2])


def block_columns(count):
    target = 2048
    if count <= target:
        return count
    best = 1
    for option in range(1, target + 1):
        if count % option == 0:
            best = option
    return best


def per_device(queries, passages, labels, projection):
    query_part = jnp.dot(queries, projection, preferred_element_type=jnp.float32)
    passage_part = jnp.dot(passages, projection, preferred_element_type=jnp.float32)
    rows = query_part.shape[0]
    embed = query_part.shape[1]
    query_embed = lax.psum(query_part, "mp").astype(jnp.bfloat16)
    passage_embed = lax.psum_scatter(
        passage_part.astype(jnp.bfloat16), "mp", scatter_dimension=0, tiled=True
    )
    offset = lax.axis_index("mp") * passage_embed.shape[0]
    width = passage_embed.shape[0]
    start_state = (
        jnp.full((rows,), -jnp.inf, jnp.float32),
        jnp.zeros((rows,), jnp.float32),
        jnp.zeros((rows,), jnp.float32),
    )
    piece = lax.all_gather(passage_embed, "dp", axis=0, tiled=True)
    count = piece.shape[0]
    columns_each = block_columns(count)
    blocks = piece.reshape(count // columns_each, columns_each, embed)
    firsts = jnp.arange(blocks.shape[0], dtype=jnp.int32) * columns_each

    def step(state, item):
        block, first = item
        scores = lax.dot_general(
            query_embed, block, (((1,), (1,)), ((), ())), preferred_element_type=jnp.float32
        )
        columns = first + lax.iota(jnp.int32, columns_each)
        passage_ids = columns // width * rows + offset + columns % width
        hit = passage_ids[None, :] == labels[:, None]
        chosen = jnp.sum(jnp.where(hit, scores, 0.0), axis=1)
        block_top = jnp.max(scores, axis=1)
        block_sum = jnp.sum(jnp.exp(scores - block_top[:, None]), axis=1)
        return (combine_stats(state, (block_top, block_sum, chosen)), None)

    result, unused = lax.scan(step, start_state, (blocks, firsts))
    top, total, chosen = merged(result, "mp", combine_stats)
    loss = top + jnp.log(total) - chosen
    return (loss, query_embed)


def solution(mesh):
    return jax.shard_map(
        per_device,
        mesh=mesh,
        in_specs=(P("dp", "mp"), P("dp", "mp"), P("dp"), P("mp", None)),
        out_specs=(P("dp"), P("dp", None)),
        check_vma=False,
    )
```

profile of v0, /device:TPU:0, one launch (start us, length us, event | category | flops | bytes accessed | tf_op | source)
XLA Modules:
  0.0 88.4 jit_solution(6473758463576834238)
XLA Ops:
  7.2 0.0 copy-start
  7.2 0.0 reduce-scatter.2.cloned.1.call-start
  7.2 1.2 %copy-done = bf16[512,1024]{1,0:T(8,128)(2,1)S(1)} copy-done((bf16[512,1024]{1,0:T(8,128)(2,1)S(1)}, bf16[512,1024]{1,0:T(8,128)(2,1)}, u32[]{:S(2)}) %copy-start) | copy-done | bytes 1048600
  8.4 2.0 %convolution_convert_fusion = bf16[512,128]{1,0:T(8,128)(2,1)} fusion(bf16[512,1024]{1,0:T(8,128)(2,1)S(1)} %copy-done, bf16[1024,128]{1,0:T(8,128)(2,1)} %param.9), kind=kOutput, calls=%fused_computation.6 | convolution fusion | flops 134283264 | bytes 1441792 | tf_op jit(solution)/shard_map/dot_general | solution.py:37
  10.4 0.0 reduce-scatter.2.cloned.1.call-update
  10.4 0.0 copy-start.2
  10.5 1.7 %fusion.11 = f32[512,128]{1,0:T(8,128)S(1)} fusion(bf16[512,1024]{1,0:T(8,128)(2,1)} %param.6, bf16[1024,128]{1,0:T(8,128)(2,1)} %param.9), kind=kOutput, calls=%fused_computation.27 | convolution fusion | flops 134217728 | bytes 1572864 | tf_op jit(solution)/shard_map/dot_general | solution.py:36
  12.2 16.3 %all-reduce.1 = bf16[512,128]{1,0:T(8,128)(2,1)S(1)} all-reduce(f32[512,128]{1,0:T(8,128)S(1)} %fusion.11), channel_id=1, replica_groups=mesh['dp'=8,'mp'=4] {'mp'}, use_global_device_ids=true, to_apply=%region_0.0 | all-reduce | flops 65536 | bytes 393216 | tf_op jit(solution)/shard_map/psum | solution.py:40
  28.5 0.0 copy-start.1
  28.5 4.5 %reduce-scatter.2.cloned.1.call-done = bf16[128,128]{1,0:T(8,128)(2,1)} async-done(((bf16[512,128]{1,0:T(8,128)(2,1)}), bf16[128,128]{1,0:T(8,128)(2,1)}) %reduce-scatter.2.cloned.1.call-update) | async-done | bytes 32784 | tf_op jit(solution)/shard_map/reduce_scatter | solution.py:41
  33.0 31.0 %all_gather.19 = bf16[1024,128]{1,0:T(8,128)(2,1)S(1)} all-gather(bf16[128,128]{1,0:T(8,128)(2,1)} %reduce-scatter.2.cloned.1.call-done), channel_id=1, replica_groups=mesh['dp'=8,'mp'=4] {'dp'}, dimensions={0}, use_global_device_ids=true | all-gather | bytes 294912 | tf_op jit(solution)/shard_map/all_gather | solution.py:51
  64.0 0.5 fusion.10
  64.5 0.0 copy-done.2
  64.5 0.7 select_reduce_fusion
  65.2 0.0 copy-done.1
  65.2 5.2 %all-gather.3 = f32[4,1,512]{2,1,0:T(1,128)S(1)} all-gather(f32[1,1,512]{2,1,0:T(1,128)S(1)} %bitcast.40), channel_id=1, replica_groups=mesh['dp'=8,'mp'=4] {'mp'}, dimensions={0}, use_global_device_ids=true | all-gather | bytes 10240 | tf_op jit(solution)/shard_map/all_gather | solution.py:8
  70.4 5.2 %all-gather.4 = f32[4,1,512]{2,1,0:T(1,128)S(1)} all-gather(f32[1,1,512]{2,1,0:T(1,128)S(1)} %bitcast.41), channel_id=3, replica_groups=mesh['dp'=8,'mp'=4] {'mp'}, dimensions={0}, use_global_device_ids=true | all-gather | bytes 10240 | tf_op jit(solution)/shard_map/all_gather | solution.py:8
  75.6 5.2 %all-gather.2 = f32[4,1,512]{2,1,0:T(1,128)S(1)} all-gather(f32[1,1,512]{2,1,0:T(1,128)S(1)} %bitcast.39), channel_id=2, replica_groups=mesh['dp'=8,'mp'=4] {'mp'}, dimensions={0}, use_global_device_ids=true | all-gather | bytes 10240 | tf_op jit(solution)/shard_map/all_gather | solution.py:8
  80.7 0.2 while.12
  81.0 0.6 add_subtract_fusion
  (20 shorter events, 0.2 us)
Async XLA Ops:
  7.2 1.2 %copy-start = (bf16[512,1024]{1,0:T(8,128)(2,1)S(1)}, bf16[512,1024]{1,0:T(8,128)(2,1)}, u32[]{:S(2)}) copy-start(bf16[512,1024]{1,0:T(8,128)(2,1)} %param.7) | copy-start | bytes 3145732
  7.2 25.8 %reduce-scatter.2.cloned.1.call-start = ((), (), s32[]{:S(2)}) async-start(), calls=%async_computation.1 | async-start | bytes 163840 | tf_op jit(solution)/shard_map/reduce_scatter | solution.py:41
  10.4 54.0 %copy-start.2 = (s32[512]{0:T(512)S(1)}, s32[512]{0:T(512)}, u32[]{:S(2)}) copy-start(s32[512]{0:T(512)} %param.8) | copy-start | bytes 6148
  28.5 36.7 %copy-start.1 = (bf16[512,128]{1,0:T(8,128)(2,1)}, bf16[512,128]{1,0:T(8,128)(2,1)S(1)}, u32[]{:S(2)}) copy-start(bf16[512,128]{1,0:T(8,128)(2,1)S(1)} %all-reduce.1) | copy-start | bytes 393220
Sparse Core Ops, SparseCore 0:
  10.6 22.3 reduce-scatter.1
where the time goes:
time: 88.7 us; the launch traced here: 88.4 us
  blocking collectives  62.8 us (71%)
  between operations  14.1 us (16%)
  waiting for transfers between devices  4.51 us (5%)
  matrix products  4.24 us (5%)
  other arithmetic  1.37 us (2%)
  local copies, waits for them, and re-layouts  1.26 us (1%)
    all_gather x1, blocking collectives, per_device(): piece = lax.all_gather(passage_embed, 'dp', axis=0, tiled=True)  31 us
    psum x1, blocking collectives, per_device(): query_embed = lax.psum(query_part, 'mp').astype(jnp.bfloat16)  16.3 us
    all_gather x3, blocking collectives, merged(): gathered = jax.tree.map(lambda a: lax.all_gather(a, axis), part)  15.5 us
    reduce_scatter x1, waiting for transfers between devices, per_device(): lax.psum_scatter(passage_part.astype(jnp.bfloat16), 'mp', scatter_dimensi...  4.5 us
    dot_general x1, matrix products, per_device(): jnp.dot(passages, projection, preferred_element_type=jnp.float32)  2.03 us
  transfers between devices with their start and end apart: 1, of which 1 were waited for; matrix products, arithmetic and copies ran while one was open for 2% of the time, Pallas kernels for 0%

commit v1 on v0

--- a/solution.py
+++ b/solution.py
@@ -48,7 +48,18 @@
         jnp.zeros((rows,), jnp.float32),
         jnp.zeros((rows,), jnp.float32),
     )
-    piece = lax.all_gather(passage_embed, "dp", axis=0, tiled=True)
+    total_devices = lax.psum(1, "dp")
+    w_next = [(nth - 1, nth) for nth in range(1, total_devices)] + [(total_devices - 1, 0)]
+    small = passage_embed
+    inbox = [small]
+    for _ in range(total_devices - 1):
+        small = lax.ppermute(small, "dp", perm=w_next)
+        inbox += [small]
+    piece = jnp.roll(
+        jnp.concatenate([*reversed(inbox)], axis=0),
+        shift=(lax.axis_index("dp") + 1) * small.shape[0],
+        axis=0,
+    )
     count = piece.shape[0]
     columns_each = block_columns(count)
     blocks = piece.reshape(count // columns_each, columns_each, embed)

time: 88.7 us -> 112 us (1.26)
  waiting for transfers between devices: 4.51 us -> 59.6 us
  blocking collectives: 62.8 us -> 29.2 us
  starting transfers between devices: 0.04 us -> 1.57 us
    ppermute x0 -> x7, waiting for transfers between devices: none -> 36.7 us  [per_device(): small = lax.ppermute(small, 'dp', perm=w_next)]
    all_gather x1 -> x0, blocking collectives: 31 us -> none  [per_device(): piece = lax.all_gather(passage_embed, 'dp', axis=0, tiled=True)]
    reduce_scatter x1, waiting for transfers between devices: 4.5 us -> 22.9 us  [per_device(): lax.psum_scatter(passage_part.astype(jnp.bfloat16), 'mp', scatter_dimensi...]
    psum x1, blocking collectives: 16.3 us -> 13.7 us  [per_device(): query_embed = lax.psum(query_part, 'mp').astype(jnp.bfloat16)]
    ppermute x0 -> x7, starting transfers between devices: none -> 1.53 us  [per_device(): small = lax.ppermute(small, 'dp', perm=w_next)]
  transfers between devices with their start and end apart: 1 -> 8, of which waited for: 1 -> 7; matrix products, arithmetic and copies ran while one was open for 2% -> 2% of each run, Pallas kernels for 0% -> 0%
where the time goes in v1:
time: 112 us
  waiting for transfers between devices  59.6 us (53%)
  blocking collectives  29.2 us (26%)
  between operations  14.2 us (13%)
  matrix products  4.27 us (4%)
  starting transfers between devices  1.57 us (1%)
  local copies, waits for them, and re-layouts  1.43 us (1%)
  other arithmetic  1.37 us (1%)
    ppermute x7, waiting for transfers between devices, per_device(): small = lax.ppermute(small, 'dp', perm=w_next)  36.7 us
    reduce_scatter x1, waiting for transfers between devices, per_device(): lax.psum_scatter(passage_part.astype(jnp.bfloat16), 'mp', scatter_dimensi...  22.9 us
    all_gather x3, blocking collectives, merged(): gathered = jax.tree.map(lambda a: lax.all_gather(a, axis), part)  15.5 us
    psum x1, blocking collectives, per_device(): query_embed = lax.psum(query_part, 'mp').astype(jnp.bfloat16)  13.7 us
  transfers between devices with their start and end apart: 8, of which 7 were waited for; matrix products, arithmetic and copies ran while one was open for 2% of the time, Pallas kernels for 0%

profile of v1, /device:TPU:0, one launch (start us, length us, event | category | flops | bytes accessed | tf_op | source)
XLA Modules:
  0.0 111.8 jit_solution(1221890776886086560)
XLA Ops:
  7.2 0.0 copy-start
  7.2 0.0 reduce-scatter.2.cloned.1.call-start
  7.2 1.2 %copy-done = bf16[512,1024]{1,0:T(8,128)(2,1)S(1)} copy-done((bf16[512,1024]{1,0:T(8,128)(2,1)S(1)}, bf16[512,1024]{1,0:T(8,128)(2,1)}, u32[]{:S(2)}) %copy-start) | copy-done | bytes 1048600
  8.4 2.0 %convolution_convert_fusion = bf16[512,128]{1,0:T(8,128)(2,1)} fusion(bf16[512,1024]{1,0:T(8,128)(2,1)S(1)} %copy-done, bf16[1024,128]{1,0:T(8,128)(2,1)} %param.9), kind=kOutput, calls=%fused_computation.6 | convolution fusion | flops 134283264 | bytes 1441792 | tf_op jit(solution)/shard_map/dot_general | solution.py:37
  10.4 0.0 reduce-scatter.2.cloned.1.call-update
  10.5 22.9 %reduce-scatter.2.cloned.1.call-done = bf16[128,128]{1,0:T(8,128)(2,1)} async-done(((bf16[512,128]{1,0:T(8,128)(2,1)}), bf16[128,128]{1,0:T(8,128)(2,1)}) %reduce-scatter.2.cloned.1.call-update) | async-done | bytes 32784 | tf_op jit(solution)/shard_map/reduce_scatter | solution.py:41
  33.4 0.0 copy-start.2
  33.4 1.5 %collective-permute-start = (bf16[128,128]{1,0:T(8,128)(2,1)}, bf16[128,128]{1,0:T(8,128)(2,1)S(1)}, u32[]{:S(2)}, u32[]{:S(2)}) collective-permute-start(bf16[128,128]{1,0:T(8,128)(2,1)} %reduce-scatter.2.cloned.1.call-done), channel_id=1, source_target_pairs={{0,4},{4,8},{8,12},{12,16},{16,20},{20,24},{24,28},{28,0},{1,5},{5... | collective-permute-start | bytes 98312 | tf_op jit(solution)/shard_map/ppermute | solution.py:56
  34.8 5.4 %collective-permute-done = bf16[128,128]{1,0:T(8,128)(2,1)S(1)} collective-permute-done((bf16[128,128]{1,0:T(8,128)(2,1)}, bf16[128,128]{1,0:T(8,128)(2,1)S(1)}, u32[]{:S(2)}, u32[]{:S(2)}) %collective-permute-start) | collective-permute-done | bytes 32800 | tf_op jit(solution)/shard_map/ppermute | solution.py:56
  40.2 0.0 collective-permute-start.1
  40.2 6.6 %collective-permute-done.1 = bf16[128,128]{1,0:T(8,128)(2,1)S(1)} collective-permute-done((bf16[128,128]{1,0:T(8,128)(2,1)S(1)}, bf16[128,128]{1,0:T(8,128)(2,1)S(1)}, u32[]{:S(2)}, u32[]{:S(2)}) %collective-permute-start.1) | collective-permute-done | bytes 32800 | tf_op jit(solution)/shard_map/ppermute | solution.py:56
  46.8 0.0 collective-permute-start.2
  46.8 6.6 %collective-permute-done.2 = bf16[128,128]{1,0:T(8,128)(2,1)S(1)} collective-permute-done((bf16[128,128]{1,0:T(8,128)(2,1)S(1)}, bf16[128,128]{1,0:T(8,128)(2,1)S(1)}, u32[]{:S(2)}, u32[]{:S(2)}) %collective-permute-start.2) | collective-permute-done | bytes 32800 | tf_op jit(solution)/shard_map/ppermute | solution.py:56
  53.4 0.0 collective-permute-start.3
  53.4 6.6 %collective-permute-done.3 = bf16[128,128]{1,0:T(8,128)(2,1)S(1)} collective-permute-done((bf16[128,128]{1,0:T(8,128)(2,1)S(1)}, bf16[128,128]{1,0:T(8,128)(2,1)S(1)}, u32[]{:S(2)}, u32[]{:S(2)}) %collective-permute-start.3) | collective-permute-done | bytes 32800 | tf_op jit(solution)/shard_map/ppermute | solution.py:56
  60.1 0.0 collective-permute-start.4
  60.1 1.7 %fusion.14 = f32[512,128]{1,0:T(8,128)S(1)} fusion(bf16[512,1024]{1,0:T(8,128)(2,1)} %param.6, bf16[1024,128]{1,0:T(8,128)(2,1)} %param.9), kind=kOutput, calls=%fused_computation.46 | convolution fusion | flops 134217728 | bytes 1572864 | tf_op jit(solution)/shard_map/dot_general | solution.py:36
  61.8 0.0 copy-start.3
  61.8 4.9 %collective-permute-done.4 = bf16[128,128]{1,0:T(8,128)(2,1)S(1)} collective-permute-done((bf16[128,128]{1,0:T(8,128)(2,1)S(1)}, bf16[128,128]{1,0:T(8,128)(2,1)S(1)}, u32[]{:S(2)}, u32[]{:S(2)}) %collective-permute-start.4) | collective-permute-done | bytes 32800 | tf_op jit(solution)/shard_map/ppermute | solution.py:56
  66.7 0.0 collective-permute-start.5
  66.7 13.7 %all-reduce.1 = bf16[512,128]{1,0:T(8,128)(2,1)S(1)} all-reduce(f32[512,128]{1,0:T(8,128)S(1)} %fusion.14), channel_id=1, replica_groups=mesh['dp'=8,'mp'=4] {'mp'}, use_global_device_ids=true, to_apply=%region_0.0 | all-reduce | flops 65536 | bytes 393216 | tf_op jit(solution)/shard_map/psum | solution.py:40
  80.4 0.0 copy-start.1
  80.4 0.0 collective-permute-done.5
  80.4 0.1 collective-permute-start.6
  80.5 6.6 %collective-permute-done.6 = bf16[128,128]{1,0:T(8,128)(2,1)S(1)} collective-permute-done((bf16[128,128]{1,0:T(8,128)(2,1)S(1)}, bf16[128,128]{1,0:T(8,128)(2,1)S(1)}, u32[]{:S(2)}, u32[]{:S(2)}) %collective-permute-start.6) | collective-permute-done | bytes 32800 | tf_op jit(solution)/shard_map/ppermute | solution.py:56
  87.2 0.0 copy-done.2
  87.3 0.5 fusion.13
  87.8 0.0 copy-done.3
  87.8 0.7 select_reduce_fusion
  88.5 0.0 copy-done.1
  88.5 5.2 %all-gather.3 = f32[4,1,512]{2,1,0:T(1,128)S(1)} all-gather(f32[1,1,512]{2,1,0:T(1,128)S(1)} %bitcast.39), channel_id=1, replica_groups=mesh['dp'=8,'mp'=4] {'mp'}, dimensions={0}, use_global_device_ids=true | all-gather | bytes 10240 | tf_op jit(solution)/shard_map/all_gather | solution.py:8
  93.7 5.2 %all-gather.4 = f32[4,1,512]{2,1,0:T(1,128)S(1)} all-gather(f32[1,1,512]{2,1,0:T(1,128)S(1)} %bitcast.40), channel_id=3, replica_groups=mesh['dp'=8,'mp'=4] {'mp'}, dimensions={0}, use_global_device_ids=true | all-gather | bytes 10240 | tf_op jit(solution)/shard_map/all_gather | solution.py:8
  98.9 5.2 %all-gather.2 = f32[4,1,512]{2,1,0:T(1,128)S(1)} all-gather(f32[1,1,512]{2,1,0:T(1,128)S(1)} %bitcast.38), channel_id=2, replica_groups=mesh['dp'=8,'mp'=4] {'mp'}, dimensions={0}, use_global_device_ids=true | all-gather | bytes 10240 | tf_op jit(solution)/shard_map/all_gather | solution.py:8
  104.1 0.2 while.12
  104.4 0.6 add_subtract_fusion
  (36 shorter events, 0.3 us)
Async XLA Ops:
  7.2 1.2 %copy-start = (bf16[512,1024]{1,0:T(8,128)(2,1)S(1)}, bf16[512,1024]{1,0:T(8,128)(2,1)}, u32[]{:S(2)}) copy-start(bf16[512,1024]{1,0:T(8,128)(2,1)} %param.7) | copy-start | bytes 3145732
  7.2 26.2 %reduce-scatter.2.cloned.1.call-start = ((), (), s32[]{:S(2)}) async-start(), calls=%async_computation.1 | async-start | bytes 163840 | tf_op jit(solution)/shard_map/reduce_scatter | solution.py:41
  33.4 53.8 %copy-start.2 = (bf16[128,128]{1,0:T(8,128)(2,1)S(1)}, bf16[128,128]{1,0:T(8,128)(2,1)}, u32[]{:S(2)}) copy-start(bf16[128,128]{1,0:T(8,128)(2,1)} %reduce-scatter.2.cloned.1.call-done) | copy-start | bytes 98308
  33.4 6.8 %collective-permute-start = (bf16[128,128]{1,0:T(8,128)(2,1)}, bf16[128,128]{1,0:T(8,128)(2,1)S(1)}, u32[]{:S(2)}, u32[]{:S(2)}) collective-permute-start(bf16[128,128]{1,0:T(8,128)(2,1)} %reduce-scatter.2.cloned.1.call-done), channel_id=1, source_target_pairs={{0,4},{4,8},{8,12},{12,16},{16,20},{20,24},{24,28},{28,0},{1,5},{5... | collective-permute-start | bytes 98312 | tf_op jit(solution)/shard_map/ppermute | solution.py:56
  40.2 6.6 %collective-permute-start.1 = (bf16[128,128]{1,0:T(8,128)(2,1)S(1)}, bf16[128,128]{1,0:T(8,128)(2,1)S(1)}, u32[]{:S(2)}, u32[]{:S(2)}) collective-permute-start(bf16[128,128]{1,0:T(8,128)(2,1)S(1)} %collective-permute-done), channel_id=1, source_target_pairs={{0,4},{4,8},{8,12},{12,16},{16,20},{20,24},{24,28},{28,0},{1,5},{5... | collective-permute-start | bytes 98312 | tf_op jit(solution)/shard_map/ppermute | solution.py:56
  46.8 6.6 %collective-permute-start.2 = (bf16[128,128]{1,0:T(8,128)(2,1)S(1)}, bf16[128,128]{1,0:T(8,128)(2,1)S(1)}, u32[]{:S(2)}, u32[]{:S(2)}) collective-permute-start(bf16[128,128]{1,0:T(8,128)(2,1)S(1)} %collective-permute-done.1), channel_id=1, source_target_pairs={{0,4},{4,8},{8,12},{12,16},{16,20},{20,24},{24,28},{28,0},{1,5},{5... | collective-permute-start | bytes 98312 | tf_op jit(solution)/shard_map/ppermute | solution.py:56
  53.4 6.6 %collective-permute-start.3 = (bf16[128,128]{1,0:T(8,128)(2,1)S(1)}, bf16[128,128]{1,0:T(8,128)(2,1)S(1)}, u32[]{:S(2)}, u32[]{:S(2)}) collective-permute-start(bf16[128,128]{1,0:T(8,128)(2,1)S(1)} %collective-permute-done.2), channel_id=1, source_target_pairs={{0,4},{4,8},{8,12},{12,16},{16,20},{20,24},{24,28},{28,0},{1,5},{5... | collective-permute-start | bytes 98312 | tf_op jit(solution)/shard_map/ppermute | solution.py:56
  60.1 6.6 %collective-permute-start.4 = (bf16[128,128]{1,0:T(8,128)(2,1)S(1)}, bf16[128,128]{1,0:T(8,128)(2,1)S(1)}, u32[]{:S(2)}, u32[]{:S(2)}) collective-permute-start(bf16[128,128]{1,0:T(8,128)(2,1)S(1)} %collective-permute-done.3), channel_id=1, source_target_pairs={{0,4},{4,8},{8,12},{12,16},{16,20},{20,24},{24,28},{28,0},{1,5},{5... | collective-permute-start | bytes 98312 | tf_op jit(solution)/shard_map/ppermute | solution.py:56
  61.8 26.1 %copy-start.3 = (s32[512]{0:T(512)S(1)}, s32[512]{0:T(512)}, u32[]{:S(2)}) copy-start(s32[512]{0:T(512)} %param.8) | copy-start | bytes 6148
  66.7 13.7 %collective-permute-start.5 = (bf16[128,128]{1,0:T(8,128)(2,1)S(1)}, bf16[128,128]{1,0:T(8,128)(2,1)S(1)}, u32[]{:S(2)}, u32[]{:S(2)}) collective-permute-start(bf16[128,128]{1,0:T(8,128)(2,1)S(1)} %collective-permute-done.4), channel_id=1, source_target_pairs={{0,4},{4,8},{8,12},{12,16},{16,20},{20,24},{24,28},{28,0},{1,5},{5... | collective-permute-start | bytes 98312 | tf_op jit(solution)/shard_map/ppermute | solution.py:56
  80.4 8.1 %copy-start.1 = (bf16[512,128]{1,0:T(8,128)(2,1)}, bf16[512,128]{1,0:T(8,128)(2,1)S(1)}, u32[]{:S(2)}) copy-start(bf16[512,128]{1,0:T(8,128)(2,1)S(1)} %all-reduce.1) | copy-start | bytes 393220
  80.4 6.7 %collective-permute-start.6 = (bf16[128,128]{1,0:T(8,128)(2,1)S(1)}, bf16[128,128]{1,0:T(8,128)(2,1)S(1)}, u32[]{:S(2)}, u32[]{:S(2)}) collective-permute-start(bf16[128,128]{1,0:T(8,128)(2,1)S(1)} %collective-permute-done.5), channel_id=1, source_target_pairs={{0,4},{4,8},{8,12},{12,16},{16,20},{20,24},{24,28},{28,0},{1,5},{5... | collective-permute-start | bytes 98312 | tf_op jit(solution)/shard_map/ppermute | solution.py:56
Sparse Core Ops, SparseCore 0:
  11.0 22.3 reduce-scatter.1
